TPU v7x, 256 devices: a whole 4x4x8 slice. The times are simulated.
256 devices in a mesh: blk: 128 (over x, z, y), rep: 2 (over core).
Axes of the slice: x: 4, y: 4, z: 8, core: 2. Of those that a mesh axis runs over, the one named last changes fastest.
Arguments:
- item_factors: bfloat16 [262144, 256], P('blk')
- user_factors: float32 [2048, 256], P(('blk', 'rep'))
- item_lists: int32 [2048, 128], P(('blk', 'rep')), may hold values from 0 to 262143, as said below
- counts: int32 [2048], P(('blk', 'rep')), may hold values from 16 to 112, as said below
- plays: int32 [2048, 128], P(('blk', 'rep')), may hold values from 0 to 999
Outputs:
- new_factors: float32 [2048, 256], P(('blk', 'rep'))
- residual_norms: float32 [4], replicated
Inputs may be any that keep to these rules, and one draw needn't show every extreme that they name: `item_lists`: entries are global item rows; index b of blk holds rows b * 2048 to (b + 1) * 2048 - 1. Among the live slots of the users of one device, at most 8 name rows held by one index of blk, and in every draw some index of blk is named by exactly 8 live slots of every device. The padding slots of one device name rows of every index of blk exactly 4 times. Slots at or after counts[u] are padding. The 8 users of one device have 8 * 64 live slots in all.
All inputs are finite; a program needn't handle non-finite values.
Results may differ from a plain program's by a relative error of at most 0.0003.
Values may be sent and summed in bfloat16 or wider, within the bound.
A program may use at most 64 MiB of HBM per device.

v0:
```python
import jax
import jax.numpy as jnp
from jax import lax
from jax.sharding import Mesh
from jax.sharding import PartitionSpec as P

ITERS = 3
BLK_REP = ("blk_0", "blk_1", "blk_2", "rep")
BLK = ("blk_0", "blk_1", "blk_2")
conf_scale = 40.0
ridge = 1.0
tiny = 1e-06


def over_axes(array, axes):
    for axis in axes:
        array = lax.psum(array, axis)
    return array


def split_up(array, dim, devices):
    dims = array.shape
    pieces = array.reshape(*dims[:dim], devices, dims[dim] // devices, *dims[dim + 1 :])
    return jnp.moveaxis(pieces, dim, 0)


def laid_out(pieces, dim):
    dims = list(pieces.shape[1:])
    dims[dim] *= pieces.shape[0]
    return jnp.moveaxis(pieces, 0, dim).reshape(dims)


def moved_by_axis(pieces, axes, sequence):
    dims = [lax.axis_size(a) for a in axes]
    pieces = pieces.reshape(*dims, *pieces.shape[1:])
    for k in sequence:
        pieces = lax.all_to_all(pieces, axes[k], split_axis=k, concat_axis=k, tiled=True)
    return pieces.reshape(-1, *pieces.shape[len(axes) :])


def exchange_by_axis(array, axes, sequence, split_dim, concat_dim):
    pieces = split_up(array, split_dim, lax.axis_size(axes))
    return laid_out(moved_by_axis(pieces, axes, sequence), concat_dim)


def operator_apply(vector, gram, item_rows, extra_weight):
    along = jnp.einsum(
        "ulk,uk->ul",
        item_rows,
        vector,
        precision=lax.Precision.HIGHEST,
        preferred_element_type=jnp.float32,
    )
    back = jnp.einsum(
        "ul,ulk->uk",
        extra_weight * along,
        item_rows,
        precision=lax.Precision.HIGHEST,
        preferred_element_type=jnp.float32,
    )
    return jnp.dot(vector, gram, precision=lax.Precision.HIGHEST) + back + ridge * vector


def global_squares(value):
    return over_axes(value, BLK_REP)


def pack_requests(owner_key, local, blocks, capacity):
    slot_total = owner_key.shape[0]
    order = jnp.argsort(owner_key, stable=True)
    sorted_owner = owner_key[order]
    starts = jnp.searchsorted(sorted_owner, jnp.arange(blocks + 1, dtype=jnp.int32))
    rank_sorted = jnp.arange(slot_total, dtype=jnp.int32) - starts[sorted_owner]
    place_sorted = jnp.where(
        sorted_owner < blocks, sorted_owner * capacity + rank_sorted, blocks * capacity
    )
    place = jnp.zeros((slot_total,), jnp.int32).at[order].set(place_sorted)
    requests = jnp.zeros((blocks * capacity + 1,), jnp.int32).at[place].set(local)
    requests = requests[: blocks * capacity].reshape(blocks, capacity)
    return (requests, jnp.minimum(place, blocks * capacity - 1))


def body(item_factors, user_factors, item_lists, counts, plays):
    own_rows, width = item_factors.shape
    user_count, list_len = item_lists.shape
    blocks = lax.axis_size(BLK)
    slot_total = user_count * list_len
    half_rows = own_rows // lax.axis_size("rep")
    mine = lax.dynamic_slice_in_dim(item_factors, lax.axis_index("rep") * half_rows, half_rows, 0)
    partial_gram = lax.dot_general(
        mine, mine, (((0,), (0,)), ((), ())), preferred_element_type=jnp.float32
    )
    gram = over_axes(partial_gram, BLK_REP)
    live = jnp.arange(list_len, dtype=jnp.int32)[None, :] < counts[:, None]
    flat_ids = item_lists.reshape(slot_total)
    owner = flat_ids // own_rows
    local = flat_ids % own_rows
    capacity = 3 * slot_total // (2 * blocks)
    requests, place = pack_requests(owner, local, blocks, capacity)
    found = item_factors[exchange_by_axis(requests, BLK, (0, 1, 2), 0, 0)]
    reply = lax.all_to_all(found, BLK, split_axis=0, concat_axis=0, tiled=True)
    item_rows = reply.reshape(blocks * capacity, width)[place].reshape(user_count, list_len, width)
    confidence = 1.0 + conf_scale * jnp.log(2.0 + plays.astype(jnp.float32))
    full_weight = jnp.where(live, confidence, jnp.float32(0.0))
    extra_weight = jnp.where(live, confidence - 1.0, jnp.float32(0.0))
    target = jnp.einsum(
        "ul,ulk->uk",
        full_weight,
        item_rows,
        precision=lax.Precision.HIGHEST,
        preferred_element_type=jnp.float32,
    )
    solution = user_factors
    residual = target - operator_apply(solution, gram, item_rows, extra_weight)
    direction = residual
    squares = jnp.sum(residual * residual, axis=1)
    collected = [jnp.sum(squares)]
    for _ in range(ITERS):
        image = operator_apply(direction, gram, item_rows, extra_weight)
        alpha = squares / (jnp.sum(direction * image, axis=1) + tiny)
        solution = solution + alpha[:, None] * direction
        residual = residual - alpha[:, None] * image
        fresh = jnp.sum(residual * residual, axis=1)
        direction = residual + (fresh / (squares + tiny))[:, None] * direction
        squares = fresh
        collected.append(jnp.sum(squares))
    totals = jnp.stack([global_squares(value) for value in collected])
    users_total = user_count * lax.axis_size(BLK) * lax.axis_size("rep")
    return (solution, jnp.sqrt(totals / (users_total * width)))


def solution(mesh):
    split = Mesh(
        mesh.devices.reshape(4, 8, 4, mesh.shape["rep"]), ("blk_0", "blk_1", "blk_2", "rep")
    )
    in_specs = (P(BLK, None), P(BLK_REP, None), P(BLK_REP, None), P(BLK_REP), P(BLK_REP, None))
    out_specs = (P(BLK_REP, None), P())
    return jax.shard_map(body, mesh=split, in_specs=in_specs, out_specs=out_specs, check_vma=False)
```

profile of v0, /device:TPU:1, one launch (start us, length us, event | category | flops | bytes accessed | tf_op | source)
XLA Modules:
  0.0 366.3 jit_solution(18274535382460058586)
XLA Ops:
  8.0 4.4 %sort.17 = (s32[1024]{0:T(1024)}, s32[1024]{0:T(1024)S(1)}) sort(s32[1024]{0:T(1024)S(1)} %get-tuple-element.128, s32[1024]{0:T(1024)S(1)} %iota.14), dimensions={0}, to_apply=%region_0.0 | sort | flops 10240 | bytes 16384 | tf_op jit(solution)/shard_map/jit(argsort)/sort | solution.py:70
  12.4 4.5 %gather_fusion.1 = s32[1024]{0:T(1024)S(1)} fusion(s32[1024]{0:T(1024)S(1)} %get-tuple-element.128, s32[1024]{0:T(1024)S(1)} %get-tuple-element.129), kind=kCustom, calls=%fused_computation.1 | custom fusion | bytes 12288 | tf_op jit(solution)/shard_map/gather | solution.py:71
  16.9 13.7 %while.24 = (s32[]{:T(128)}, u32[129]{0:T(256)S(1)}, u32[129]{0:T(256)S(1)}, s32[1024]{0:T(1024)S(1)}, s32[]{:T(128)}, /*index=5*/s32[]{:T(128)}, s32[]{}) while((s32[]{:T(128)}, u32[129]{0:T(256)S(1)}, u32[129]{0:T(256)S(1)}, s32[1024]{0:T(1024)S(1)}, s32[]{:T(128)}, /*index=5*/s32[]{:T(128)}, s32[]{}) %tuple.51), condition=%wide.region_2.0_spmd.clone, body=%wide.region_1.0_spmd.clone.sunk | while | flops 2705 | bytes 10388 | solution.py:72
  17.0 1.2 gather_fusion
  18.2 1.2 gather_fusion
  19.4 1.2 gather_fusion
  20.7 1.2 gather_fusion
  21.9 1.2 gather_fusion
  23.2 1.2 gather_fusion
  24.4 1.2 gather_fusion
  25.6 1.2 gather_fusion
  28.1 1.2 gather_fusion
  29.4 1.2 gather_fusion
  30.6 6.8 %gather_fusion.2 = s32[1024]{0:T(1024)S(1)} fusion(s32[129]{0:T(256)S(1)} %convert_element_type.14, s32[1024]{0:T(1024)S(1)} %broadcast_clamp_fusion), kind=kCustom, calls=%fused_computation.2 | custom fusion | bytes 12288 | tf_op jit(solution)/shard_map/gather | solution.py:73
  37.4 4.3 %scatter_custom_fusion = s32[1024]{0:T(1024)S(1)} fusion(s32[1024]{0:T(1024)S(1)} %get-tuple-element.130, s32[1024]{0:T(1024)S(1)} %add_select_fusion.2, s32[]{:T(128)} %constant.80.clone.1), kind=kCustom, calls=%fused_computation.76 | custom fusion | bytes 4100 | tf_op jit(solution)/shard_map/scatter | solution.py:77
  41.8 4.3 %scatter_custom_fusion.1 = s32[1537]{0:T(1024)S(1)} fusion(s32[1024]{0:T(1024)S(1)} %get-tuple-element.126, s32[1024]{0:T(1024)S(1)} %get-tuple-element.127, s32[]{:T(128)} %constant.80.clone.1), kind=kCustom, calls=%fused_computation.66 | custom fusion | bytes 6152 | tf_op jit(solution)/shard_map/scatter | solution.py:78
  46.4 8.8 %all_to_all.20 = s32[4,1,384]{2,1,0:T(1,128)S(1)} all-to-all(s32[4,1,384]{2,1,0:T(1,128)S(1)} %reshape.175), channel_id=1, replica_groups=mesh['blk_0'=4,'blk_1'=8,'blk_2'=4,'rep'=2] {'blk_0'}, dimensions={0} | all-to-all | bytes 12288 | tf_op jit(solution)/shard_map/all_to_all | solution.py:37
  56.6 14.6 %all_to_all.21 = s32[8,1,192]{2,1,0:T(1,128)S(1)} all-to-all(s32[8,1,192]{2,1,0:T(1,128)S(1)} %reshape.177), channel_id=1, replica_groups=mesh['blk_0'=4,'blk_1'=8,'blk_2'=4,'rep'=2] {'blk_1'}, dimensions={0} | all-to-all | bytes 12288 | tf_op jit(solution)/shard_map/all_to_all | solution.py:37
  72.1 8.1 %all_to_all.22 = s32[4,1,384]{2,1,0:T(1,128)S(1)} all-to-all(s32[4,1,384]{2,1,0:T(1,128)S(1)} %reshape.179), channel_id=1, replica_groups=mesh['blk_0'=4,'blk_1'=8,'blk_2'=4,'rep'=2] {'blk_2'}, dimensions={0} | all-to-all | bytes 12288 | tf_op jit(solution)/shard_map/all_to_all | solution.py:37
  81.3 4.8 %gather_fusion.3 = bf16[1536,256]{1,0:T(8,128)(2,1)S(1)} fusion(bf16[2048,256]{1,0:T(8,128)(2,1)S(1)} %copy-done, s32[2048]{0:T(1024)S(1)} %pad_clamp_fusion.1), kind=kCustom, calls=%fused_computation.3 | custom fusion | bytes 1579008 | tf_op jit(solution)/shard_map/gather | solution.py:100
  87.2 6.2 %all-to-all-start.3 = ((bf16[128,12,256]{2,1,0:T(8,128)(2,1)}), bf16[128,12,256]{2,1,0:T(8,128)(2,1)S(1)}, u32[]{:S(2)}, u32[]{:S(2)}) async-start(bf16[128,12,256]{2,1,0:T(8,128)(2,1)} %reshape.113), calls=%async_computation.3 | async-start | bytes 2097152 | tf_op jit(solution)/shard_map/all_to_all | solution.py:101
  94.6 52.2 %all-reduce.9.cloned.1.call-done = f32[256,256]{1,0:T(8,128)} async-done(((f32[256,256]{1,0:T(8,128)}), f32[256,256]{1,0:T(8,128)}) %all-reduce.9.cloned.1.call-update) | async-done | bytes 262160 | tf_op jit(solution)/shard_map/psum | solution.py:17
  146.9 72.6 %all-reduce.11.cloned.1.call-done = f32[256,256]{1,0:T(8,128)} async-done(((f32[256,256]{1,0:T(8,128)}), f32[256,256]{1,0:T(8,128)}) %all-reduce.11.cloned.1.call-update) | async-done | bytes 262160 | tf_op jit(solution)/shard_map/psum | solution.py:17
  219.6 50.7 %all-reduce.13.cloned.1.call-done = f32[256,256]{1,0:T(8,128)} async-done(((f32[256,256]{1,0:T(8,128)}), f32[256,256]{1,0:T(8,128)}) %all-reduce.13.cloned.1.call-update) | async-done | bytes 262160 | tf_op jit(solution)/shard_map/psum | solution.py:17
  270.5 3.9 %gather_fusion.4 = bf16[1024,256]{1,0:T(8,128)(2,1)S(1)} fusion(bf16[1536,256]{1,0:T(8,128)(2,1)S(1)} %reshape.86, s32[1024]{0:T(1024)S(1)} %get-tuple-element.125), kind=kCustom, calls=%fused_computation.4 | custom fusion | bytes 1052672 | tf_op jit(solution)/shard_map/gather | solution.py:102
  276.4 28.7 %all-reduce.15.cloned.1.call-done = f32[256,256]{1,0:T(8,128)} async-done(((f32[256,256]{1,0:T(8,128)}), f32[256,256]{1,0:T(8,128)}) %all-reduce.15.cloned.1.call-update) | async-done | bytes 262160 | tf_op jit(solution)/shard_map/psum | solution.py:17
  312.2 1.3 multiply_reduce_fusion.4
  313.5 8.8 %all-reduce.2 = (f32[]{:T(128)}, f32[]{:T(128)}, f32[]{:T(128)}, f32[]{:T(128)}) all-reduce(f32[]{:T(128)} %get-tuple-element.93, f32[]{:T(128)} %get-tuple-element.92, f32[]{:T(128)} %get-tuple-element.90, f32[]{:T(128)} %get-tuple-element.87), channel_id=1, replica_groups=mesh['blk_0'=4,'blk_1'=8,'blk_2'=4,'rep'=2] {'blk_0'}, use_global_device_ids=true, to_apply=%region_31.32 | all-reduce | flops 4 | bytes 32 | tf_op jit(solution)/shard_map/psum | solution.py:17
  322.3 14.4 %all-reduce = (f32[]{:T(128)}, f32[]{:T(128)}, f32[]{:T(128)}, f32[]{:T(128)}) all-reduce(f32[]{:T(128)} %get-tuple-element.110, f32[]{:T(128)} %get-tuple-element.111, f32[]{:T(128)} %get-tuple-element.112, f32[]{:T(128)} %get-tuple-element.113), channel_id=1, replica_groups=mesh['blk_0'=4,'blk_1'=8,'blk_2'=4,'rep'=2] {'blk_1'}, use_global_device_ids=true, to_apply=%region_32.33 | all-reduce | flops 4 | bytes 32 | tf_op jit(solution)/shard_map/psum | solution.py:17
  336.7 9.1 %all-reduce.1 = (f32[]{:T(128)}, f32[]{:T(128)}, f32[]{:T(128)}, f32[]{:T(128)}) all-reduce(f32[]{:T(128)} %get-tuple-element.102, f32[]{:T(128)} %get-tuple-element.103, f32[]{:T(128)} %get-tuple-element.104, f32[]{:T(128)} %get-tuple-element.105), channel_id=1, replica_groups=mesh['blk_0'=4,'blk_1'=8,'blk_2'=4,'rep'=2] {'blk_2'}, use_global_device_ids=true, to_apply=%region_33.34 | all-reduce | flops 4 | bytes 32 | tf_op jit(solution)/shard_map/psum | solution.py:17
  345.9 10.9 %all-reduce.3 = (f32[1]{0:T(128)}, f32[1]{0:T(128)}, f32[1]{0:T(128)}, f32[1]{0:T(128)}) all-reduce(f32[1]{0:T(128)} %bitcast.36, f32[1]{0:T(128)} %bitcast.35, f32[1]{0:T(128)} %bitcast.34, f32[1]{0:T(128)} %bitcast.33), channel_id=1, replica_groups=mesh['blk_0'=4,'blk_1'=8,'blk_2'=4,'rep'=2] {'rep'}, use_global_device_ids=true, to_apply=%region_34.35 | all-reduce | flops 4 | bytes 32 | tf_op jit(solution)/shard_map/psum | solution.py:17
  356.7 3.0 fusion.29
  (109 shorter events, 17.4 us)
Async XLA Ops:
  7.2 74.1 %copy-start = (bf16[2048,256]{1,0:T(8,128)(2,1)S(1)}, bf16[2048,256]{1,0:T(8,128)(2,1)}, u32[]{:S(2)}) copy-start(bf16[2048,256]{1,0:T(8,128)(2,1)} %param.7) | copy-start | bytes 3145732
  87.2 183.1 %all-to-all-start.3 = ((bf16[128,12,256]{2,1,0:T(8,128)(2,1)}), bf16[128,12,256]{2,1,0:T(8,128)(2,1)S(1)}, u32[]{:S(2)}, u32[]{:S(2)}) async-start(bf16[128,12,256]{2,1,0:T(8,128)(2,1)} %reshape.113), calls=%async_computation.3 | async-start | bytes 2097152 | tf_op jit(solution)/shard_map/all_to_all | solution.py:101
  93.4 53.4 %all-reduce.9.cloned.1.call-start = ((), (), s32[]{:S(2)}) async-start(), calls=%async_computation.4 | async-start | bytes 524288 | tf_op jit(solution)/shard_map/psum | solution.py:17
  94.5 125.0 %all-reduce.11.cloned.1.call-start = ((), (), s32[]{:S(2)}) async-start(), calls=%async_computation.5 | async-start | bytes 524288 | tf_op jit(solution)/shard_map/psum | solution.py:17
  146.8 123.5 %all-reduce.13.cloned.1.call-start = ((), (), s32[]{:S(2)}) async-start(), calls=%async_computation.6 | async-start | bytes 524288 | tf_op jit(solution)/shard_map/psum | solution.py:17
  219.5 85.6 %all-reduce.15.cloned.1.call-start = ((), (), s32[]{:S(2)}) async-start(), calls=%async_computation.7 | async-start | bytes 524288 | tf_op jit(solution)/shard_map/psum | solution.py:17
  270.5 4.0 %copy-start.2 = (f32[8,256]{1,0:T(8,128)S(1)}, f32[8,256]{1,0:T(8,128)}, u32[]{:S(2)}) copy-start(f32[8,256]{1,0:T(8,128)} %param.8) | copy-start | bytes 24580
  274.5 0.7 copy-start.3
  275.0 0.7 copy-start.4
  306.9 1.0 copy-start.1
Sparse Core Ops, SparseCore 0:
  96.5 50.2 all-reduce.8
  149.1 70.3 all-reduce.10
  221.9 48.3 all-reduce.12
  272.7 32.3 all-reduce.14
where the time goes:
time: 367 us; the launch traced here: 366 us
  waiting for transfers between devices  204 us (56%)
  blocking collectives  74.7 us (20%)
  local copies, waits for them, and re-layouts  45.8 us (12%)
  between operations  14.1 us (4%)
  other arithmetic  13.2 us (4%)
  matrix products  7.29 us (2%)
  starting transfers between devices  6.35 us (2%)
    psum x4, waiting for transfers between devices, over_axes(): array = lax.psum(array, axis)  204 us
    psum x4, blocking collectives, over_axes(): array = lax.psum(array, axis)  43.2 us
    all_to_all x3, blocking collectives, moved_by_axis(): lax.all_to_all(pieces, axes[k], split_axis=k, concat_axis=k, tiled=True)  31.5 us
    gather x11, local copies, waits for them, and re-layouts, pack_requests(): jnp.searchsorted(sorted_owner, jnp.arange(blocks + 1, dtype=jnp.int32))  12.9 us
  transfers between devices with their start and end apart: 5, of which 4 were waited for; matrix products, arithmetic and copies ran while one was open for 2% of the time, Pallas kernels for 0%

commit v1 on v0

--- a/solution.py
+++ b/solution.py
@@ -14,7 +14,7 @@
 
 def over_axes(array, axes):
     for axis in axes:
-        array = lax.psum(array, axis)
+        array = jnp.sum(lax.all_gather(array, axis), axis=0)
     return array
 
 

time: 367 us -> 246 us (0.67)
  waiting for transfers between devices: 204 us -> 45.7 us
  local copies, waits for them, and re-layouts: 45.8 us -> 71.1 us
  other arithmetic: 13.2 us -> 28.9 us
    psum x4 -> x0, waiting for transfers between devices: 204 us -> none  [over_axes(): array = lax.psum(array, axis)]
    psum x4 -> x0, blocking collectives: 43.2 us -> none  [over_axes(): array = lax.psum(array, axis)]
    unnamed x0 -> x4, blocking collectives: none -> 38.7 us
    all_gather x0 -> x3, waiting for transfers between devices: none -> 27.4 us  [over_axes(): array = jnp.sum(lax.all_gather(array, axis), axis=0)]
    unnamed x17 -> x59, local copies, waits for them, and re-layouts: 2.05 us -> 27.4 us
    all_to_all x1, waiting for transfers between devices: 0.01 us -> 18.3 us  [body(): reply = lax.all_to_all(found, BLK, split_axis=0, concat_axis=0, tiled=True)]
    reduce_sum x0 -> x20, other arithmetic: none -> 15.6 us  [over_axes(): array = jnp.sum(lax.all_gather(array, axis), axis=0)]
    all_gather x0 -> x1, blocking collectives: none -> 4.2 us  [over_axes(): array = jnp.sum(lax.all_gather(array, axis), axis=0)]
  transfers between devices with their start and end apart: 5 -> 4, of which waited for: 4 -> 3; matrix products, arithmetic and copies ran while one was open for 2% -> 23% of each run, Pallas kernels for 0% -> 0%
where the time goes in v1:
time: 246 us; the launch traced here: 245 us
  blocking collectives  71.5 us (29%)
  local copies, waits for them, and re-layouts  71.1 us (29%)
  waiting for transfers between devices  45.7 us (19%)
  other arithmetic  28.9 us (12%)
  between operations  14.2 us (6%)
  starting transfers between devices  6.44 us (3%)
  matrix products  6.36 us (3%)
    unnamed x4, blocking collectives  38.7 us
    all_to_all x3, blocking collectives, moved_by_axis(): lax.all_to_all(pieces, axes[k], split_axis=k, concat_axis=k, tiled=True)  28.6 us
    unnamed x59, local copies, waits for them, and re-layouts  27.4 us
    all_gather x3, waiting for transfers between devices, over_axes(): array = jnp.sum(lax.all_gather(array, axis), axis=0)  27.4 us
    all_to_all x1, waiting for transfers between devices, body(): reply = lax.all_to_all(found, BLK, split_axis=0, concat_axis=0, tiled=True)  18.3 us
    reduce_sum x20, other arithmetic, over_axes(): array = jnp.sum(lax.all_gather(array, axis), axis=0)  15.6 us
    gather x11, local copies, waits for them, and re-layouts, pack_requests(): jnp.searchsorted(sorted_owner, jnp.arange(blocks + 1, dtype=jnp.int32))  12.9 us
    gather x1, local copies, waits for them, and re-layouts, pack_requests(): rank_sorted = jnp.arange(slot_total, dtype=jnp.int32) - starts[sorted_owner]  6.83 us
  transfers between devices with their start and end apart: 4, of which 3 were waited for; matrix products, arithmetic and copies ran while one was open for 23% of the time, Pallas kernels for 0%

profile of v1, /device:TPU:1, one launch (start us, length us, event | category | flops | bytes accessed | tf_op | source)
XLA Modules:
  0.0 244.6 jit_solution(10830549447623414149)
XLA Ops:
  10.2 4.4 %sort.17 = (s32[1024]{0:T(1024)}, s32[1024]{0:T(1024)S(1)}) sort(s32[1024]{0:T(1024)S(1)} %get-tuple-element.128, s32[1024]{0:T(1024)S(1)} %iota.14), dimensions={0}, to_apply=%region_0.0 | sort | flops 10240 | bytes 16384 | tf_op jit(solution)/shard_map/jit(argsort)/sort | solution.py:70
  14.6 4.5 %gather_fusion.1 = s32[1024]{0:T(1024)S(1)} fusion(s32[1024]{0:T(1024)S(1)} %get-tuple-element.128, s32[1024]{0:T(1024)S(1)} %get-tuple-element.129), kind=kCustom, calls=%fused_computation.1 | custom fusion | bytes 12288 | tf_op jit(solution)/shard_map/gather | solution.py:71
  19.2 19.0 %all-gather.8.cloned.1.call-done = f32[1024,256]{1,0:T(8,128)} async-done(((f32[256,256]{1,0:T(8,128)}), f32[1024,256]{1,0:T(8,128)}) %all-gather.8.cloned.1.call-update) | async-done | bytes 1048592 | tf_op jit(solution)/shard_map/all_gather | solution.py:17
  38.2 2.0 reduce_sum.274
  40.2 13.7 %while.24 = (s32[]{:T(128)}, u32[129]{0:T(256)S(1)}, u32[129]{0:T(256)S(1)}, s32[1024]{0:T(1024)S(1)}, s32[]{:T(128)}, /*index=5*/s32[]{:T(128)}, s32[]{}) while((s32[]{:T(128)}, u32[129]{0:T(256)S(1)}, u32[129]{0:T(256)S(1)}, s32[1024]{0:T(1024)S(1)}, s32[]{:T(128)}, /*index=5*/s32[]{:T(128)}, s32[]{}) %tuple.51), condition=%wide.region_2.0_spmd.clone, body=%wide.region_1.0_spmd.clone.sunk | while | flops 2705 | bytes 10396 | solution.py:72
  53.9 6.8 %gather_fusion.2 = s32[1024]{0:T(1024)S(1)} fusion(s32[129]{0:T(256)S(1)} %convert_element_type.14, s32[1024]{0:T(1024)S(1)} %broadcast_clamp_fusion), kind=kCustom, calls=%fused_computation.2 | custom fusion | bytes 12288 | tf_op jit(solution)/shard_map/gather | solution.py:73
  60.8 4.3 %scatter_custom_fusion = s32[1024]{0:T(1024)S(1)} fusion(s32[1024]{0:T(1024)S(1)} %get-tuple-element.130, s32[1024]{0:T(1024)S(1)} %add_select_fusion.2, s32[]{:T(128)} %constant.80.clone.1), kind=kCustom, calls=%fused_computation.76 | custom fusion | bytes 4100 | tf_op jit(solution)/shard_map/scatter | solution.py:77
  65.1 4.3 %scatter_custom_fusion.1 = s32[1537]{0:T(1024)S(1)} fusion(s32[1024]{0:T(1024)S(1)} %get-tuple-element.126, s32[1024]{0:T(1024)S(1)} %get-tuple-element.127, s32[]{:T(128)} %constant.80.clone.1), kind=kCustom, calls=%fused_computation.66 | custom fusion | bytes 6152 | tf_op jit(solution)/shard_map/scatter | solution.py:78
  69.7 7.7 %all_to_all.20 = s32[4,1,384]{2,1,0:T(1,128)S(1)} all-to-all(s32[4,1,384]{2,1,0:T(1,128)S(1)} %reshape.259), channel_id=1, replica_groups=mesh['blk_0'=4,'blk_1'=8,'blk_2'=4,'rep'=2] {'blk_0'}, dimensions={0} | all-to-all | bytes 12288 | tf_op jit(solution)/shard_map/all_to_all | solution.py:37
  78.8 13.0 %all_to_all.21 = s32[8,1,192]{2,1,0:T(1,128)S(1)} all-to-all(s32[8,1,192]{2,1,0:T(1,128)S(1)} %reshape.261), channel_id=1, replica_groups=mesh['blk_0'=4,'blk_1'=8,'blk_2'=4,'rep'=2] {'blk_1'}, dimensions={0} | all-to-all | bytes 12288 | tf_op jit(solution)/shard_map/all_to_all | solution.py:37
  92.8 8.0 %all_to_all.22 = s32[4,1,384]{2,1,0:T(1,128)S(1)} all-to-all(s32[4,1,384]{2,1,0:T(1,128)S(1)} %reshape.263), channel_id=1, replica_groups=mesh['blk_0'=4,'blk_1'=8,'blk_2'=4,'rep'=2] {'blk_2'}, dimensions={0} | all-to-all | bytes 12288 | tf_op jit(solution)/shard_map/all_to_all | solution.py:37
  101.7 4.8 %gather_fusion.3 = bf16[1536,256]{1,0:T(8,128)(2,1)S(1)} fusion(bf16[2048,256]{1,0:T(8,128)(2,1)S(1)} %copy-done, s32[2048]{0:T(1024)S(1)} %pad_clamp_fusion.1), kind=kCustom, calls=%fused_computation.3 | custom fusion | bytes 1579008 | tf_op jit(solution)/shard_map/gather | solution.py:100
  107.7 6.3 %all-to-all-start.3 = ((bf16[128,12,256]{2,1,0:T(8,128)(2,1)}), bf16[128,12,256]{2,1,0:T(8,128)(2,1)S(1)}, u32[]{:S(2)}, u32[]{:S(2)}) async-start(bf16[128,12,256]{2,1,0:T(8,128)(2,1)} %reshape.113), calls=%async_computation.3 | async-start | bytes 2097152 | tf_op jit(solution)/shard_map/all_to_all | solution.py:101
  114.1 2.5 %reduce_sum.275 = f32[256,256]{1,0:T(8,128)} reduce(f32[8,256,256]{2,1,0:T(8,128)} %bitcast.149, f32[]{:T(128)} %constant.79.clone.1), dimensions={0}, to_apply=%region_6.7 | reduce | flops 458752 | bytes 2359300 | tf_op jit(solution)/shard_map/reduce_sum | solution.py:17
  117.3 18.3 %all-to-all-done.3 = bf16[128,12,256]{2,1,0:T(8,128)(2,1)S(1)} async-done(((bf16[128,12,256]{2,1,0:T(8,128)(2,1)}), bf16[128,12,256]{2,1,0:T(8,128)(2,1)S(1)}, u32[]{:S(2)}, u32[]{:S(2)}) %all-to-all-start.3) | async-done | bytes 786464 | tf_op jit(solution)/shard_map/all_to_all | solution.py:101
  135.8 3.9 %gather_fusion.4 = bf16[1024,256]{1,0:T(8,128)(2,1)S(1)} fusion(bf16[1536,256]{1,0:T(8,128)(2,1)S(1)} %reshape.86, s32[1024]{0:T(1024)S(1)} %get-tuple-element.125), kind=kCustom, calls=%fused_computation.4 | custom fusion | bytes 1052672 | tf_op jit(solution)/shard_map/gather | solution.py:102
  140.9 8.3 %all-gather.12.cloned.1.call-done = f32[1024,256]{1,0:T(8,128)} async-done(((f32[256,256]{1,0:T(8,128)}), f32[1024,256]{1,0:T(8,128)}) %all-gather.12.cloned.1.call-update) | async-done | bytes 1048592 | tf_op jit(solution)/shard_map/all_gather | solution.py:17
  150.6 4.2 %all-gather.3 = f32[512,256]{1,0:T(8,128)S(1)} all-gather(f32[256,256]{1,0:T(8,128)S(1)} %reduce_sum.276), channel_id=5, replica_groups=mesh['blk_0'=4,'blk_1'=8,'blk_2'=4,'rep'=2] {'rep'}, dimensions={0}, use_global_device_ids=true | all-gather | bytes 786432 | tf_op jit(solution)/shard_map/all_gather | solution.py:17
  164.5 1.5 dynamic-update-slice.4
  166.0 1.4 dynamic-update-slice
  168.1 8.2 %all-reduce.18 = (f32[4]{0:T(128)S(1)}, f32[4]{0:T(128)S(1)}, f32[4]{0:T(128)S(1)}, f32[4]{0:T(128)S(1)}) all-reduce(f32[4]{0:T(128)S(1)} %dynamic-update-slice.12, f32[4]{0:T(128)S(1)} %dynamic-update-slice.8, f32[4]{0:T(128)S(1)} %dynamic-update-slice.4, ...), channel_id=1, replica_groups=mesh['blk_0'=4,'blk_1'=8,'blk_2'=4,'rep'=2] {'blk_0'}, use_global_device_ids=true, to_apply=%add.12 | all-reduce | flops 16 | bytes 128
  177.5 1.4 dynamic-update-slice.13
  180.9 1.4 dynamic-update-slice.5
  182.9 1.4 dynamic-update-slice.1
  185.0 13.3 %all-reduce.16 = (f32[8]{0:T(128)S(1)}, f32[8]{0:T(128)S(1)}, f32[8]{0:T(128)S(1)}, f32[8]{0:T(128)S(1)}) all-reduce(f32[8]{0:T(128)S(1)} %dynamic-update-slice.13, f32[8]{0:T(128)S(1)} %dynamic-update-slice.9, f32[8]{0:T(128)S(1)} %dynamic-update-slice.5, ...), channel_id=1, replica_groups=mesh['blk_0'=4,'blk_1'=8,'blk_2'=4,'rep'=2] {'blk_1'}, use_global_device_ids=true, to_apply=%add.13 | all-reduce | flops 32 | bytes 256
  199.5 1.4 dynamic-update-slice.14
  202.9 1.4 dynamic-update-slice.6
  207.1 6.9 %all-reduce.17 = (f32[4]{0:T(128)S(1)}, f32[4]{0:T(128)S(1)}, f32[4]{0:T(128)S(1)}, f32[4]{0:T(128)S(1)}) all-reduce(f32[4]{0:T(128)S(1)} %dynamic-update-slice.14, f32[4]{0:T(128)S(1)} %dynamic-update-slice.10, f32[4]{0:T(128)S(1)} %dynamic-update-slice.6, ...), channel_id=1, replica_groups=mesh['blk_0'=4,'blk_1'=8,'blk_2'=4,'rep'=2] {'blk_2'}, use_global_device_ids=true, to_apply=%add.14 | all-reduce | flops 16 | bytes 128
  215.2 1.4 dynamic-update-slice.15
  220.7 1.4 dynamic-update-slice.3
  222.1 10.3 %all-reduce.19 = (f32[2]{0:T(128)S(1)}, f32[2]{0:T(128)S(1)}, f32[2]{0:T(128)S(1)}, f32[2]{0:T(128)S(1)}) all-reduce(f32[2]{0:T(128)S(1)} %dynamic-update-slice.15, f32[2]{0:T(128)S(1)} %dynamic-update-slice.11, f32[2]{0:T(128)S(1)} %dynamic-update-slice.7, ...), channel_id=1, replica_groups=mesh['blk_0'=4,'blk_1'=8,'blk_2'=4,'rep'=2] {'rep'}, use_global_device_ids=true, to_apply=%add.15 | all-reduce | flops 8 | bytes 64
  235.0 3.1 %fusion.29 = f32[4]{0:T(128)} fusion(f32[1]{0:T(128)} %bitcast.60, f32[1]{0:T(128)} %bitcast.55, f32[1]{0:T(128)} %bitcast.50, f32[1]{0:T(128)} %bitcast.45), kind=kLoop, calls=%fused_computation.79 | loop fusion | flops 16 | bytes 32 | tf_op jit(solution)/shard_map/sqrt | solution.py:129
  (169 shorter events, 52.8 us)
Async XLA Ops:
  7.2 1.2 copy-start
  7.2 31.0 %all-gather.8.cloned.1.call-start = ((), (), s32[]{:S(2)}) async-start(), calls=%async_computation.4 | async-start | bytes 1310720 | tf_op jit(solution)/shard_map/all_gather | solution.py:17
  9.5 104.6 %all-gather.10.cloned.1.call-start = ((), (), s32[]{:S(2)}) async-start(), calls=%async_computation.5 | async-start | bytes 2359296 | tf_op jit(solution)/shard_map/all_gather | solution.py:17
  107.7 8.9 %copy-start.7 = (u32[256]{0:T(256)S(1)}, u32[256]{0:T(256)}, u32[]{:S(2)}) copy-start(u32[256]{0:T(256)} %constant.104) | copy-start | bytes 3076
  107.7 27.9 %all-to-all-start.3 = ((bf16[128,12,256]{2,1,0:T(8,128)(2,1)}), bf16[128,12,256]{2,1,0:T(8,128)(2,1)S(1)}, u32[]{:S(2)}, u32[]{:S(2)}) async-start(bf16[128,12,256]{2,1,0:T(8,128)(2,1)} %reshape.113), calls=%async_computation.3 | async-start | bytes 2097152 | tf_op jit(solution)/shard_map/all_to_all | solution.py:101
  114.0 35.3 %all-gather.12.cloned.1.call-start = ((), (), s32[]{:S(2)}) async-start(), calls=%async_computation.6 | async-start | bytes 1310720 | tf_op jit(solution)/shard_map/all_gather | solution.py:17
  135.7 4.0 %copy-start.1 = (f32[8,256]{1,0:T(8,128)S(1)}, f32[8,256]{1,0:T(8,128)}, u32[]{:S(2)}) copy-start(f32[8,256]{1,0:T(8,128)} %param.8) | copy-start | bytes 24580
  135.7 4.5 %copy-start.2 = (s32[8,128]{1,0:T(8,128)S(1)}, s32[8,128]{1,0:T(8,128)}, u32[]{:S(2)}) copy-start(s32[8,128]{1,0:T(8,128)} %param.11) | copy-start | bytes 12292
  135.7 4.5 %copy-start.3 = (s32[8]{0:T(128)S(1)}, s32[8]{0:T(128)}, u32[]{:S(2)}) copy-start(s32[8]{0:T(128)} %param.10) | copy-start | bytes 100
  155.1 12.4 %copy-start.6 = (u32[256]{0:T(256)S(1)}, u32[256]{0:T(256)}, u32[]{:S(2)}) copy-start(u32[256]{0:T(256)} %constant.109) | copy-start | bytes 3076
  155.1 29.3 %copy-start.5 = (u32[256]{0:T(256)S(1)}, u32[256]{0:T(256)}, u32[]{:S(2)}) copy-start(u32[256]{0:T(256)} %constant.114) | copy-start | bytes 3076
  155.1 51.3 %copy-start.4 = (u32[256]{0:T(256)S(1)}, u32[256]{0:T(256)}, u32[]{:S(2)}) copy-start(u32[256]{0:T(256)} %constant.119) | copy-start | bytes 3076
Sparse Core Ops, SparseCore 0:
  9.8 28.3 all-gather.7
  40.4 39.0 all-gather.9
  116.7 32.5 all-gather.11
